TPU v7x, 32 devices: a whole 2x2x4 slice. The times are simulated.
32 devices in a mesh: srv: 16 (over z, y, x), grp: 2 (over core).
Axes of the slice: x: 2, y: 2, z: 4, core: 2. Of those that a mesh axis runs over, the one named last changes fastest.
Arguments:
- basis_modes: float32 [64, 64, 3072], P(None, ('srv', 'grp')), may hold values from -10 to 10
- weights: float32 [64], replicated, may hold values from 0.5 to 4
- snapshots: float32 [16, 64, 3072], P(None, 'srv', 'grp'), may hold values from -10 to 10
Outputs:
- new_modes: float32 [80, 64, 3072], P(None, ('srv', 'grp'))
- factor: float32 [80, 80], replicated
All inputs are finite; a program needn't handle non-finite values.
Results may differ from a plain program's by a relative error of at most 0.00009.
Values sent between devices are 32-bit elements; how exact they have to be, the bound alone decides.
No kernel may reach another device: no remote copies, remote signals or barrier semaphores. Data moves between devices by JAX's collectives and lax.ppermute only.
A program may use at most 64 MiB of HBM per device.

v0:
```python
import jax
import jax.numpy as jnp
from jax import lax
from jax.sharding import PartitionSpec as P

MODES = 64
SNAPS = 16


def merged_factor(local_gram):
    return jnp.linalg.cholesky(lax.psum(local_gram, ("srv", "grp")))


def per_device(basis_modes, weights, snapshots):
    width = MODES + SNAPS
    total_cells = (
        basis_modes.shape[1] * basis_modes.shape[2] * lax.axis_size("srv") * lax.axis_size("grp")
    )
    scaled = basis_modes * weights[:, None, None]
    arrived = lax.all_to_all(snapshots, "grp", split_axis=1, concat_axis=2, tiled=True)
    panel = jnp.concatenate([scaled, arrived], axis=0).reshape(width, -1)
    local_gram = (
        jnp.dot(panel, panel.T, precision=lax.Precision.HIGHEST, preferred_element_type=jnp.float32)
        / total_cells
    )
    factor = merged_factor(local_gram)
    inverse = lax.linalg.triangular_solve(
        factor, jnp.eye(width, dtype=jnp.float32), left_side=True, lower=True
    )
    result = jnp.dot(
        inverse, panel, precision=lax.Precision.HIGHEST, preferred_element_type=jnp.float32
    )
    result = result.reshape(width, basis_modes.shape[1], basis_modes.shape[2])
    return (result, factor)


def solution(mesh):
    in_specs = (P(None, ("srv", "grp"), None), P(), P(None, "srv", "grp"))
    out_specs = (P(None, ("srv", "grp"), None), P())
    return jax.shard_map(
        per_device, mesh=mesh, in_specs=in_specs, out_specs=out_specs, check_vma=False
    )
```

profile of v0, /device:TPU:0, one launch (start us, length us, event | category | flops | bytes accessed | tf_op | source)
XLA Modules:
  0.0 77.2 jit_solution(11390154502908591722)
XLA Ops:
  0.6 0.0 copy-start
  0.6 0.0 copy-start.1
  0.6 1.2 %copy.19 = f32[16,4,1536]{2,0,1:T(8,128)S(1)} copy(f32[16,4,1536]{2,1,0:T(4,128)} %param.5) | data formatting | bytes 786432 | tf_op args[2]
  1.9 4.0 %all_to_all.18 = f32[16,4,1536]{2,0,1:T(8,128)S(1)} all-to-all(f32[16,4,1536]{2,0,1:T(8,128)S(1)} %copy.19), channel_id=1, replica_groups=mesh['srv'=16,'grp'=2] {'grp'}, dimensions={1} | all-to-all | bytes 786432 | tf_op jit(solution)/shard_map/all_to_all | solution.py:20
  5.9 1.1 %copy.41 = f32[16,2,2,1536]{3,1,0,2:T(2,128)} copy(f32[16,2,2,1536]{3,0,2,1:T(8,128)S(1)} %bitcast.35) | data formatting | bytes 786432 | tf_op jit(solution)/shard_map/all_to_all | solution.py:20
  7.0 0.3 copy.42
  7.3 0.0 copy-done
  7.3 0.0 copy-done.1
  7.3 0.5 copy_multiply_fusion
  7.8 0.5 fusion.17
  8.4 2.1 %all_to_all.16 = f32[16,2,3072]{2,0,1:T(8,128)} reshape(f32[16,2,2,1536]{3,2,0,1:T(2,128)} %bitcast.38) | data formatting | bytes 786432 | tf_op jit(solution)/shard_map/all_to_all | solution.py:20
  10.4 3.4 %fusion.10 = f32[80,80]{0,1:T(8,128)} fusion(f32[16,2,3072]{2,0,1:T(8,128)} %all_to_all.16, f32[64,2,3072]{2,0,1:T(8,128)S(1)} %copy_multiply_fusion), kind=kOutput, calls=%fused_computation.11 | convolution fusion | flops 472357120 | bytes 1991680 | tf_op jit(solution)/shard_map/dot_general | solution.py:23
  13.9 42.4 %psum.7 = f32[80,80]{0,1:T(8,128)S(1)} all-reduce(f32[80,80]{0,1:T(8,128)} %fusion.10), channel_id=1, replica_groups=mesh['srv'=16,'grp'=2] {'srv','grp'}, use_global_device_ids=true, to_apply=%region_0.0 | all-reduce | flops 6400 | bytes 51200 | tf_op jit(solution)/shard_map/psum | solution.py:11
  56.2 0.1 copy.23
  56.3 7.3 %cholesky.17 = f32[80,80]{1,0:T(8,128)S(1)} custom-call(f32[80,80]{1,0:T(8,128)S(1)} %fusion.14), custom_call_target="Cholesky" | custom-call | tf_op jit(solution)/shard_map/jit(cholesky)/cholesky | solution.py:11
  63.7 0.6 compare_reduce_fusion
  64.3 1.3 %select_bitcast_fusion = (f32[1,80,80]{2,1,0:T(8,128)S(1)}, f32[80,80]{1,0:T(8,128)}) fusion(f32[80,80]{1,0:T(8,128)S(1)} %cholesky.17, pred[]{:T(512)} %compare_reduce_fusion), kind=kLoop, calls=%fused_computation.17 | loop fusion | flops 25600 | bytes 76801 | tf_op jit(solution)/shard_map/triangular_solve | solution.py:27
  65.6 6.1 %custom-call.6 = f32[1,80,80]{1,2,0:T(8,128)S(1)} custom-call(f32[1,80,80]{2,1,0:T(8,128)S(1)} %get-tuple-element.8), custom_call_target="InvertDiagBlocksLowerTriangular" | custom-call | tf_op jit(solution)/shard_map/triangular_solve | solution.py:27
  71.7 0.2 convolution_bitcast_fusion
  72.0 0.3 concatenate.12
  72.3 0.1 copy.31
  72.4 0.1 pad_maximum_fusion
  72.6 1.8 %fusion = f32[80,2,3072]{2,0,1:T(8,128)S(1)} fusion(f32[80,80,1]{1,0,2:T(8,128)S(1)} %convolution_bitcast_fusion, f32[10,2,8,3072]{3,2,1,0:T(8,128)S(1)} %bitcast.33), kind=kOutput, calls=%fused_computation | convolution fusion | flops 471859200 | bytes 3957760 | tf_op jit(solution)/shard_map/dot_general | solution.py:30
  74.4 2.8 %copy.26 = f32[80,2,3072]{2,1,0:T(2,128)} copy(f32[80,2,3072]{2,0,1:T(8,128)S(1)} %fusion) | data formatting | bytes 3932160
  (2 shorter events, 0.0 us)
Async XLA Ops:
  0.6 6.7 %copy-start = (f32[64,2,3072]{2,1,0:T(2,128)S(1)}, f32[64,2,3072]{2,1,0:T(2,128)}, u32[]{:S(2)}) copy-start(f32[64,2,3072]{2,1,0:T(2,128)} %param.3) | copy-start | bytes 4718596
  0.6 6.7 %copy-start.1 = (f32[64]{0:T(128)S(1)}, f32[64]{0:T(128)}, u32[]{:S(2)}) copy-start(f32[64]{0:T(128)} %param.4) | copy-start | bytes 772
where the time goes:
time: 77.6 us; the launch traced here: 77.2 us
  blocking collectives  46.4 us (60%)
  other arithmetic  16.6 us (21%)
  local copies, waits for them, and re-layouts  7.98 us (10%)
  matrix products  5.45 us (7%)
    psum x1, blocking collectives, merged_factor(): return jnp.linalg.cholesky(lax.psum(local_gram, ('srv', 'grp')))  42.4 us
    another operation x3, other arithmetic, merged_factor(): return jnp.linalg.cholesky(lax.psum(local_gram, ('srv', 'grp')))  7.98 us
    another operation x2, other arithmetic, per_device(): lax.linalg.triangular_solve(factor, jnp.eye(width, dtype=jnp.float32), le...  7.4 us
    all_to_all x1, blocking collectives, per_device(): lax.all_to_all(snapshots, 'grp', split_axis=1, concat_axis=2, tiled=True)  4.05 us
    unnamed x6, local copies, waits for them, and re-layouts  4.04 us
    all_to_all x3, local copies, waits for them, and re-layouts, per_device(): lax.all_to_all(snapshots, 'grp', split_axis=1, concat_axis=2, tiled=True)  3.43 us
    dot_general x1, matrix products, per_device(): jnp.dot(panel, panel.T, precision=lax.Precision.HIGHEST, preferred_elemen...  3.41 us
    dot_general x1, matrix products, per_device(): jnp.dot(inverse, panel, precision=lax.Precision.HIGHEST, preferred_elemen...  1.82 us

commit v1 on v0

--- a/solution.py
+++ b/solution.py
@@ -8,7 +8,12 @@
 
 
 def merged_factor(local_gram):
-    return jnp.linalg.cholesky(lax.psum(local_gram, ("srv", "grp")))
+
+    def cubes_put(chunk, which_axis, lane_axis):
+        aux = jax.lax.psum(chunk, which_axis)
+        return jax.lax.psum(aux, lane_axis)
+
+    return jnp.linalg.cholesky(cubes_put(local_gram, "grp", lane_axis="srv"))
 
 
 def per_device(basis_modes, weights, snapshots):

time: 77.6 us -> 118 us (1.52)
  blocking collectives: 46.4 us -> 86.8 us
    psum x1 -> x2, blocking collectives: 42.4 us -> 82.7 us  [the longest x1 78.7 us: cubes_put(): return jax.lax.psum(aux, lane_axis)]
where the time goes in v1:
time: 118 us
  blocking collectives  86.8 us (74%)
  other arithmetic  16.6 us (14%)
  local copies, waits for them, and re-layouts  7.99 us (7%)
  matrix products  5.45 us (5%)
    psum x1, blocking collectives, cubes_put(): return jax.lax.psum(aux, lane_axis)  78.7 us
    another operation x3, other arithmetic, merged_factor(): return jnp.linalg.cholesky(cubes_put(local_gram, 'grp', lane_axis='srv'))  7.98 us
    another operation x2, other arithmetic, per_device(): lax.linalg.triangular_solve(factor, jnp.eye(width, dtype=jnp.float32), le...  7.4 us
    psum x1, blocking collectives, cubes_put(): aux = jax.lax.psum(chunk, which_axis)  4.08 us
    all_to_all x1, blocking collectives, per_device(): lax.all_to_all(snapshots, 'grp', split_axis=1, concat_axis=2, tiled=True)  4.05 us
    unnamed x6, local copies, waits for them, and re-layouts  4.04 us
    all_to_all x3, local copies, waits for them, and re-layouts, per_device(): lax.all_to_all(snapshots, 'grp', split_axis=1, concat_axis=2, tiled=True)  3.43 us
    dot_general x1, matrix products, per_device(): jnp.dot(panel, panel.T, precision=lax.Precision.HIGHEST, preferred_elemen...  3.41 us

profile of v1, /device:TPU:0, one launch (start us, length us, event | category | flops | bytes accessed | tf_op | source)
XLA Modules:
  0.0 117.5 jit_solution(3051410211175186194)
XLA Ops:
  0.6 0.0 copy-start
  0.6 0.0 copy-start.1
  0.6 1.2 %copy.19 = f32[16,4,1536]{2,0,1:T(8,128)S(1)} copy(f32[16,4,1536]{2,1,0:T(4,128)} %param.5) | data formatting | bytes 786432 | tf_op args[2]
  1.9 4.0 %all_to_all.18 = f32[16,4,1536]{2,0,1:T(8,128)S(1)} all-to-all(f32[16,4,1536]{2,0,1:T(8,128)S(1)} %copy.19), channel_id=1, replica_groups=mesh['srv'=16,'grp'=2] {'grp'}, dimensions={1} | all-to-all | bytes 786432 | tf_op jit(solution)/shard_map/all_to_all | solution.py:25
  5.9 1.1 copy.41
  7.0 0.3 copy.42
  7.3 0.0 copy-done
  7.3 0.0 copy-done.1
  7.3 0.5 copy_multiply_fusion
  7.8 0.5 fusion.17
  8.4 2.1 %all_to_all.16 = f32[16,2,3072]{2,0,1:T(8,128)} reshape(f32[16,2,2,1536]{3,2,0,1:T(2,128)} %bitcast.38) | data formatting | bytes 786432 | tf_op jit(solution)/shard_map/all_to_all | solution.py:25
  10.4 3.4 %fusion.10 = f32[80,80]{0,1:T(8,128)} fusion(f32[16,2,3072]{2,0,1:T(8,128)} %all_to_all.16, f32[64,2,3072]{2,0,1:T(8,128)S(1)} %copy_multiply_fusion), kind=kOutput, calls=%fused_computation.11 | convolution fusion | flops 472357120 | bytes 1991680 | tf_op jit(solution)/shard_map/dot_general | solution.py:28
  13.9 4.1 %psum.14 = f32[80,80]{0,1:T(8,128)S(1)} all-reduce(f32[80,80]{0,1:T(8,128)} %fusion.10), channel_id=1, replica_groups=mesh['srv'=16,'grp'=2] {'grp'}, use_global_device_ids=true, to_apply=%region_0.0 | all-reduce | flops 6400 | bytes 51200 | tf_op jit(solution)/shard_map/psum | solution.py:13
  17.9 78.7 %psum.15 = f32[80,80]{0,1:T(8,128)S(1)} all-reduce(f32[80,80]{0,1:T(8,128)S(1)} %psum.14), channel_id=1, replica_groups=mesh['srv'=16,'grp'=2] {'srv'}, use_global_device_ids=true, to_apply=%region_1.0 | all-reduce | flops 6400 | bytes 51200 | tf_op jit(solution)/shard_map/psum | solution.py:14
  96.6 0.1 copy.23
  96.7 7.3 %cholesky.17 = f32[80,80]{1,0:T(8,128)S(1)} custom-call(f32[80,80]{1,0:T(8,128)S(1)} %fusion.14), custom_call_target="Cholesky" | custom-call | tf_op jit(solution)/shard_map/jit(cholesky)/cholesky | solution.py:16
  104.0 0.6 compare_reduce_fusion
  104.7 1.3 %select_bitcast_fusion = (f32[1,80,80]{2,1,0:T(8,128)S(1)}, f32[80,80]{1,0:T(8,128)}) fusion(f32[80,80]{1,0:T(8,128)S(1)} %cholesky.17, pred[]{:T(512)} %compare_reduce_fusion), kind=kLoop, calls=%fused_computation.17 | loop fusion | flops 25600 | bytes 76801 | tf_op jit(solution)/shard_map/triangular_solve | solution.py:32
  106.0 6.1 %custom-call.6 = f32[1,80,80]{1,2,0:T(8,128)S(1)} custom-call(f32[1,80,80]{2,1,0:T(8,128)S(1)} %get-tuple-element.8), custom_call_target="InvertDiagBlocksLowerTriangular" | custom-call | tf_op jit(solution)/shard_map/triangular_solve | solution.py:32
  112.1 0.2 convolution_bitcast_fusion
  112.3 0.3 concatenate.12
  112.7 0.1 copy.31
  112.8 0.1 pad_maximum_fusion
  112.9 1.8 %fusion = f32[80,2,3072]{2,0,1:T(8,128)S(1)} fusion(f32[80,80,1]{1,0,2:T(8,128)S(1)} %convolution_bitcast_fusion, f32[10,2,8,3072]{3,2,1,0:T(8,128)S(1)} %bitcast.33), kind=kOutput, calls=%fused_computation | convolution fusion | flops 471859200 | bytes 3957760 | tf_op jit(solution)/shard_map/dot_general | solution.py:35
  114.7 2.8 %copy.26 = f32[80,2,3072]{2,1,0:T(2,128)} copy(f32[80,2,3072]{2,0,1:T(8,128)S(1)} %fusion) | data formatting | bytes 3932160
  (2 shorter events, 0.0 us)
Async XLA Ops:
  0.6 6.7 %copy-start = (f32[64,2,3072]{2,1,0:T(2,128)S(1)}, f32[64,2,3072]{2,1,0:T(2,128)}, u32[]{:S(2)}) copy-start(f32[64,2,3072]{2,1,0:T(2,128)} %param.3) | copy-start | bytes 4718596
  0.6 6.7 %copy-start.1 = (f32[64]{0:T(128)S(1)}, f32[64]{0:T(128)}, u32[]{:S(2)}) copy-start(f32[64]{0:T(128)} %param.4) | copy-start | bytes 772
